TPU v7x, 32 devices: a whole 2x2x4 slice. The times are simulated.
32 devices in a mesh: grp: 2 (over y), leaf: 4 (over z), sub: 4 (over x, core).
Axes of the slice: x: 2, y: 2, z: 4, core: 2. Of those that a mesh axis runs over, the one named last changes fastest.
Arguments:
- targets: bfloat16 [64, 65536], P(None, ('grp', 'leaf', 'sub')), parts along dimension 1, may hold values from -6 to 6
- tree_order: int32 [32, 2048], P(('grp', 'leaf', 'sub')), parts along dimension 0, may hold values from 0 to 2047, each once within a row
- leaf_inverse: bfloat16 [128, 512, 512], P(('grp', 'leaf', 'sub')), parts along dimension 0, as said below
- cluster_basis: bfloat16 [6, 32, 65536], P(None, None, ('grp', 'leaf', 'sub')), parts along dimension 2, may hold values from -1.5 to 1.5
- coupling: float32 [32, 6, 32, 64], P(('grp', 'leaf', 'sub')), parts along dimension 0, may hold values from -0.75 to 0.75
- train_coords: bfloat16 [3, 65536], P(None, ('grp', 'leaf', 'sub')), parts along dimension 1, may hold values from 0 to 1
- test_coords: bfloat16 [3, 65536], P(None, ('grp', 'leaf', 'sub')), parts along dimension 1, may hold values from 0 to 1
- test_basis: bfloat16 [4, 32, 65536], P(None, None, ('grp', 'leaf', 'sub')), parts along dimension 2, may hold values from -2.4 to 2.4
- near_leaves: int32 [32, 8], P(('grp', 'leaf', 'sub')), parts along dimension 0, may hold values from 0 to 63, as said below
Outputs:
- posterior_mean: bfloat16 [64, 65536], P(None, ('grp', 'leaf', 'sub')), parts along dimension 1
There are 2 independent parts, one for each index of `grp`. A program takes and returns all parts, laid end to end along the dimension named above; each array names one. Nothing has to cross between parts.
Inputs may be any that keep to these rules, and one draw needn't show every extreme that they name: `tree_order`: row d is a permutation of the positions 0 to 2047 within panel d. `near_leaves`: row d names 8 different training leaves, all held by panels d - 1, d or d + 1. `leaf_inverse`: each block is the identity plus dense full-rank entries of spread 0.5 / sqrt(512).
All inputs are finite; a program needn't handle non-finite values.
Results may differ from a plain program's by a relative error of at most 0.0035.
Values may be sent and summed in bfloat16 or wider, within the bound.
A program may use at most 64 MiB of HBM per device.

v0:
```python
import functools
import math

import jax
import jax.numpy as jnp
from jax import lax
from jax.experimental import pallas as pl
from jax.experimental.pallas import tpu as pltpu
from jax.sharding import PartitionSpec as P

variance = 2.0
length_scale = 0.5
highest = lax.Precision.HIGHEST
f32 = jnp.float32
bf16 = jnp.bfloat16
CHUNK = 256
TILE = 1024
FEATS = 16


def nt(a, b):
    return lax.dot_general(a, b, (((1,), (1,)), ((), ())), preferred_element_type=f32)


def tn(a, b):
    return lax.dot_general(a, b, (((0,), (0,)), ((), ())), preferred_element_type=f32)


def exact(a, b):
    return lax.dot_general(
        a, b, (((1,), (0,)), ((), ())), precision=highest, preferred_element_type=f32
    )


def halves(x):
    high = x.astype(bf16)
    return high, (x - high.astype(f32)).astype(bf16)


def thirds(x):
    first = x.astype(bf16).astype(f32)
    second = (x - first).astype(bf16).astype(f32)
    return [first, second, (x - first - second).astype(bf16).astype(f32)]


def toggled(index, mask):
    bit = 1
    while bit <= mask:
        if mask & bit:
            index = index + bit - 2 * bit * lax.rem(lax.div(index, bit), 2)
        bit *= 2
    return index


def kernel(
    panels,
    sub_size,
    order_ref,
    targets_ref,
    inverse_ref,
    basis_ref,
    coupling_ref,
    train_ref,
    test_ref,
    test_basis_ref,
    near_ref,
    out_ref,
    sent,
    received,
    far_sent,
    far_received,
    coord_window,
    features,
    test_features,
    blocks,
    weight_window,
    round_send,
    round_recv,
    far_send,
    far_recv,
    coord_send,
    coord_recv,
    weight_send,
    weight_recv,
):
    columns, points = targets_ref.shape
    leaf_count, leaf_size = inverse_ref.shape[0], inverse_ref.shape[1]
    levels, rank = basis_ref.shape[0], basis_ref.shape[1]
    near = near_ref.shape[1]
    tests = test_ref.shape[1]
    local = leaf_count.bit_length() - 1
    depth = levels - local
    me = lax.axis_index("leaf") * sub_size + lax.axis_index("sub")

    def device(index):
        return {"leaf": lax.div(index, sub_size), "sub": lax.rem(index, sub_size)}

    barrier = pltpu.get_barrier_semaphore()
    for mask in range(1, panels):
        pl.semaphore_signal(
            barrier,
            inc=1,
            device_id=device(toggled(me, mask)),
            device_id_type=pl.DeviceIdType.MESH,
        )

    scale = jnp.concatenate(
        [jnp.full((rank, 1), 1.0 / math.sqrt(leaf_size << level), f32) for level in range(levels)],
        axis=0,
    )
    basis = basis_ref[...].reshape(levels * rank, points)
    coupling = [coupling_ref[0, level] for level in range(levels)]

    stacked = jnp.concatenate(
        [targets_ref[:, h * CHUNK : (h + 1) * CHUNK] for h in range(points // CHUNK)], axis=0
    )
    order = order_ref[...]
    low, high = lax.rem(order, CHUNK), lax.div(order, CHUNK)
    solved, coefs, grams, bases = [], [], [], []
    for leaf in range(leaf_count):
        span = slice(leaf * leaf_size, (leaf + 1) * leaf_size)
        places = lax.broadcasted_iota(jnp.int32, (CHUNK, leaf_size), 0)
        chosen = jnp.where(places == low[:, span], 1.0, 0.0).astype(bf16)
        picked = jnp.dot(stacked, chosen, preferred_element_type=f32)
        taken = jnp.zeros((columns, leaf_size), f32)
        for h in range(points // CHUNK):
            taken = jnp.where(
                high[:, span] == h, picked[h * columns : (h + 1) * columns], taken
            )
        state = nt(taken.astype(bf16), inverse_ref[leaf])
        leaf_basis = basis[:, span]
        state_high, state_low = halves(state)
        coefs.append((nt(leaf_basis, state_high) + nt(leaf_basis, state_low)) * scale)
        grams.append(nt(leaf_basis, leaf_basis))
        solved.append(state)
        bases.append(leaf_basis)

    mixes = [[] for _ in range(leaf_count)]
    for level in range(local):
        rows = slice(level * rank, (level + 1) * rank)
        width = 1 << level
        child = [
            sum(coefs[c * width + i][rows] for i in range(width))
            for c in range(leaf_count // width)
        ]
        mixed = [
            exact(coupling[level], jnp.concatenate([child[c], child[c ^ 1]], axis=0))
            for c in range(leaf_count // width)
        ]
        for leaf in range(leaf_count):
            mixes[leaf].append(mixed[leaf // width])
            coefs[leaf] = coefs[leaf] - scale * exact(grams[leaf][:, rows], mixed[leaf // width])

    top = local * rank
    own = sum(coef[top:] for coef in coefs)
    gram = sum(one[top:, top:] for one in grams)
    carried = [
        scale[top + (k + 1) * rank :]
        * exact(gram[(k + 1) * rank :, k * rank : (k + 1) * rank], coupling[local + k])
        for k in range(depth - 1)
    ]

    pl.semaphore_wait(barrier, panels - 1)

    def remote(source, target, send, recv, index):
        return pltpu.make_async_remote_copy(
            src_ref=source,
            dst_ref=target,
            send_sem=send,
            recv_sem=recv,
            device_id=device(index),
            device_id_type=pl.DeviceIdType.MESH,
        )

    def shared(copy_next, copy_prev):
        def start():
            pl.when(me < panels - 1)(copy_next.start)
            pl.when(me > 0)(copy_prev.start)

        def wait():
            pl.when(me < panels - 1)(copy_next.wait_send)
            pl.when(me > 0)(copy_prev.wait_send)
            pl.when(me > 0)(copy_next.wait_recv)
            pl.when(me < panels - 1)(copy_prev.wait_recv)

        return start, wait

    after, before = lax.rem(me + 1, panels), lax.rem(me + panels - 1, panels)
    start_coords, wait_coords = shared(
        remote(train_ref, coord_window.at[0], coord_send.at[0], coord_recv.at[0], after),
        remote(train_ref, coord_window.at[1], coord_send.at[1], coord_recv.at[1], before),
    )
    start_coords()

    gain = 3.0 / (length_scale * length_scale) * math.log2(math.e) ** 2

    def norm(pos):
        return gain * (pos[0:1] * pos[0:1] + pos[1:2] * pos[1:2] + pos[2:3] * pos[2:3])

    def train_side(pos):
        ones = jnp.ones((3, points), f32)
        zero = jnp.zeros((1, points), f32)
        parts = thirds(-2.0 * gain * pos) + thirds(norm(pos)) + [ones, zero]
        return jnp.concatenate(parts, axis=0).astype(bf16)

    def put_features(panel, pos):
        made = train_side(pos.astype(f32))
        for leaf in range(leaf_count):
            features[panel * leaf_count + leaf] = made[:, leaf * leaf_size : (leaf + 1) * leaf_size]

    first_leaf = (me - 1) * leaf_count

    def window_leaf(slot):
        return jnp.clip(near_ref[0, slot] - first_leaf, 0, 3 * leaf_count - 1)

    def near_block(step, carry):
        slot, tile = lax.div(step, tests // TILE), lax.rem(step, tests // TILE)
        lanes = pl.ds(pl.multiple_of(tile * TILE, TILE), TILE)
        squared = tn(features[window_leaf(slot)], test_features[:, lanes])
        squared = jnp.maximum(squared, 1e-12)
        scaled = squared * lax.rsqrt(squared)
        value = (variance + (variance * math.log(2.0)) * scaled) * jnp.exp2(-scaled)
        blocks[pl.ds(pl.multiple_of(slot * leaf_size, leaf_size), leaf_size), lanes] = value.astype(
            bf16
        )
        return carry

    total_steps = near * (tests // TILE)
    marks = [0] + [min(16, 3 * r) for r in range(1, depth + 1)]
    cuts = [total_steps * min(m, 12) // 16 for m in marks]

    lengths = []
    for r in range(depth):
        height = (depth - r) * rank
        wide = sum((depth - 1 - k) * rank for k in range(r, depth - 1))
        lengths.append(max(height, wide))
    offsets = [sum(lengths[:r]) for r in range(depth)]

    mixed_far = []
    for r in range(depth):
        height = own.shape[0]
        rows = pl.ds(offsets[r], lengths[r])
        if carried:
            packed = jnp.concatenate(carried, axis=0)
        else:
            packed = jnp.zeros((height, 2 * rank), f32)
        wide = packed.shape[0]
        left, right = own, packed
        if height < lengths[r]:
            left = jnp.concatenate([own, jnp.zeros((lengths[r] - height, columns), f32)], axis=0)
        if wide < lengths[r]:
            right = jnp.concatenate([packed, jnp.zeros((lengths[r] - wide, 2 * rank), f32)], axis=0)
        sent[rows] = jnp.concatenate([left, right], axis=1)
        copy = remote(
            sent.at[rows], received.at[rows], round_send.at[r], round_recv.at[r], toggled(me, 1 << r)
        )
        copy.start()
        if r == 0:
            test_pos = test_ref[...].astype(f32)
            ones = jnp.ones((3, tests), f32)
            zero = jnp.zeros((1, tests), f32)
            test_features[...] = jnp.concatenate(
                [test_pos, test_pos, test_pos, ones] + thirds(norm(test_pos)) + [zero], axis=0
            ).astype(bf16)
            put_features(1, train_ref[...])
        if r == min(1, depth - 1):
            wait_coords()
            put_features(0, coord_window[0])
            put_features(2, coord_window[1])
        if r >= min(1, depth - 1):
            lax.fori_loop(cuts[r - 1] if r > 1 else 0, cuts[r], near_block, 0)
        copy.wait()
        other = received[rows]
        sibling = other[:height, :columns]
        joined = jnp.concatenate([own[:rank], sibling[:rank]], axis=0)
        mixed_far.append(exact(coupling[local + r], joined))
        if r < depth - 1:
            flipped = jnp.concatenate([sibling[:rank], own[:rank]], axis=0)
            step = (depth - 1 - r) * rank
            own = (
                own[rank:]
                + sibling[rank:]
                - exact(carried[0], joined)
                - exact(other[:step, columns:], flipped)
            )
            summed = []
            for k in range(r + 1, depth - 1):
                size = (depth - 1 - k) * rank
                summed.append(carried[k - r] + other[step : step + size, columns:])
                step += size
            carried = summed

    terms = jnp.zeros((depth * rank, columns), f32)
    for leaf in range(leaf_count):
        mix = jnp.concatenate(mixes[leaf] + mixed_far, axis=0)
        mix_high, mix_low = halves(mix)
        state = solved[leaf] - tn(mix_high, bases[leaf]) - tn(mix_low, bases[leaf])
        weights = state.astype(bf16)
        weight_window[leaf_count + leaf] = weights
        terms = terms + nt(bases[leaf][top:], weights)
    panel = weight_window.at[pl.ds(leaf_count, leaf_count)]
    start_weights, wait_weights = shared(
        remote(
            panel,
            weight_window.at[pl.ds(0, leaf_count)],
            weight_send.at[0],
            weight_recv.at[0],
            after,
        ),
        remote(
            panel,
            weight_window.at[pl.ds(2 * leaf_count, leaf_count)],
            weight_send.at[1],
            weight_recv.at[1],
            before,
        ),
    )
    start_weights()
    terms = terms * scale[top:]
    half = rank // 2
    for k in range(depth):
        far_sent[k] = jnp.concatenate(
            [terms[k * rank : k * rank + half], terms[k * rank + half : (k + 1) * rank]], axis=1
        )
    far_copies = []
    for mask in range(1, panels):
        copy = remote(
            far_sent.at[mask.bit_length() - 1],
            far_received.at[mask],
            far_send.at[mask],
            far_recv.at[mask],
            toggled(me, mask),
        )
        copy.start()
        far_copies.append(copy)
    lax.fori_loop(cuts[depth - 1] if depth > 1 else 0, total_steps, near_block, 0)
    for copy in far_copies:
        copy.wait()
    far_rows = []
    for k in range(depth):
        total = sum(far_received[mask] for mask in range(1 << k, 2 << k))
        far_rows += [total[:, :columns], total[:, columns:]]
    far_high, far_low = halves(jnp.concatenate(far_rows, axis=0))
    test_basis = test_basis_ref[...].reshape(depth * rank, tests)
    wait_weights()
    held = jnp.concatenate(
        [weight_window[window_leaf(slot)] for slot in range(near)], axis=1
    )
    for tile in range(tests // TILE):
        lanes = slice(tile * TILE, (tile + 1) * TILE)
        near_sum = jnp.dot(held, blocks[:, lanes], preferred_element_type=f32)
        far_sum = tn(far_high, test_basis[:, lanes]) + tn(far_low, test_basis[:, lanes])
        out_ref[:, lanes] = (near_sum * (1.0 / math.sqrt(near * leaf_size)) + far_sum).astype(bf16)


def shards(
    panels,
    sub_size,
    targets,
    tree_order,
    leaf_inverse,
    cluster_basis,
    coupling,
    train_coords,
    test_coords,
    test_basis,
    near_leaves,
):
    columns, points = targets.shape
    leaf_count, leaf_size = leaf_inverse.shape[0], leaf_inverse.shape[1]
    levels, rank = cluster_basis.shape[0], cluster_basis.shape[1]
    near = near_leaves.shape[1]
    tests = test_coords.shape[1]
    depth = levels - (leaf_count.bit_length() - 1)
    rows = 0
    for r in range(depth):
        wide = sum((depth - 1 - k) * rank for k in range(r, depth - 1))
        rows += max((depth - r) * rank, wide)
    vmem = pl.BlockSpec(memory_space=pltpu.VMEM)
    smem = pl.BlockSpec(memory_space=pltpu.SMEM)
    sems = pltpu.SemaphoreType.DMA
    return pl.pallas_call(
        functools.partial(kernel, panels, sub_size),
        out_shape=jax.ShapeDtypeStruct((columns, tests), bf16),
        in_specs=[vmem] * 8 + [smem],
        out_specs=vmem,
        scratch_shapes=[
            pltpu.VMEM((rows, columns + 2 * rank), f32),
            pltpu.VMEM((rows, columns + 2 * rank), f32),
            pltpu.VMEM((depth, rank // 2, 2 * columns), f32),
            pltpu.VMEM((panels, rank // 2, 2 * columns), f32),
            pltpu.VMEM((2, 3, points), bf16),
            pltpu.VMEM((3 * leaf_count, FEATS, leaf_size), bf16),
            pltpu.VMEM((FEATS, tests), bf16),
            pltpu.VMEM((near * leaf_size, tests), bf16),
            pltpu.VMEM((3 * leaf_count, columns, leaf_size), bf16),
            sems((depth,)),
            sems((depth,)),
            sems((panels,)),
            sems((panels,)),
            sems((2,)),
            sems((2,)),
            sems((2,)),
            sems((2,)),
        ],
        compiler_params=pltpu.CompilerParams(
            collective_id=0, has_side_effects=True, vmem_limit_bytes=60 * 1024 * 1024
        ),
    )(
        tree_order,
        targets,
        leaf_inverse,
        cluster_basis,
        coupling,
        train_coords,
        test_coords,
        test_basis,
        near_leaves,
    )


def solution(mesh):
    return jax.shard_map(
        functools.partial(shards, mesh.shape["leaf"] * mesh.shape["sub"], mesh.shape["sub"]),
        mesh=mesh,
        in_specs=(
            P(None, ("grp", "leaf", "sub")),
            P(("grp", "leaf", "sub"), None),
            P(("grp", "leaf", "sub"), None, None),
            P(None, None, ("grp", "leaf", "sub")),
            P(("grp", "leaf", "sub"), None, None, None),
            P(None, ("grp", "leaf", "sub")),
            P(None, ("grp", "leaf", "sub")),
            P(None, None, ("grp", "leaf", "sub")),
            P(("grp", "leaf", "sub"), None),
        ),
        out_specs=P(None, ("grp", "leaf", "sub")),
        check_vma=False,
    )
```

profile of v0, /device:TPU:0, one launch (start us, length us, event | category | flops | bytes accessed | tf_op | source)
XLA Modules:
  0.0 35.5 jit_solution(10678767093088051980)
XLA Ops:
  0.0 33.8 %shard_map.91 = bf16[64,2048]{1,0:T(8,128)(2,1)} custom-call(s32[1,2048]{1,0:T(1,128)} %order_ref.1, bf16[64,2048]{1,0:T(8,128)(2,1)} %targets_ref.1, bf16[4,512,512]{2,1,0:T(8,128)(2,1)} %inverse_ref.1, bf16[6,32,2048]{2,1,0:T(8,128)(2,1)} %basis_ref.1, f32[1,6,32,64]{3,2,1,0:T(8,128)} %coupling_ref.1, bf16[3,2048]{1,0:T(4,128)(2,1)} %train_ref.1, ...), custom_call_target="tpu_custom_call" | custom-call | tf_op jit(solution)/shard_map/pallas_call | solution.py:382
  33.8 1.7 %copy.11 = bf16[64,2048]{1,0:T(8,128)(2,1)} copy(bf16[64,2048]{1,0:T(8,128)(2,1)} %shard_map.91) | data formatting | bytes 524288
where the time goes:
time: 35.6 us; the launch traced here: 35.5 us
  Pallas kernels  33.8 us (95%)
  local copies, waits for them, and re-layouts  1.67 us (5%)
    pallas_call x1, Pallas kernels, shards(): pl.pallas_call(functools.partial(kernel, panels, sub_size), out_shape=jax...  33.8 us
    unnamed x1, local copies, waits for them, and re-layouts  1.67 us

commit v1 on v0

v1 whole, which is shorter than its diff:
```python
import functools
import math

import jax
import jax.numpy as jnp
from jax import lax
from jax.experimental import pallas as pl
from jax.experimental.pallas import tpu as pltpu
from jax.sharding import PartitionSpec as P

variance = 2.0
length_scale = 0.5
f32 = jnp.float32
bf16 = jnp.bfloat16
CHUNK = 256
TILE = 1024
FEATS = 16
EARLY = 7


def nt(a, b):
    return lax.dot_general(a, b, (((1,), (1,)), ((), ())), preferred_element_type=f32)


def nn(a, b):
    return jnp.dot(a, b, preferred_element_type=f32)


def tn(a, b):
    return lax.dot_general(a, b, (((0,), (0,)), ((), ())), preferred_element_type=f32)


def halves(x):
    high = x.astype(bf16)
    return high, (x - high.astype(f32)).astype(bf16)


def thirds(x):
    first = x.astype(bf16).astype(f32)
    second = (x - first).astype(bf16).astype(f32)
    return [first, second, (x - first - second).astype(bf16).astype(f32)]


def toggled(index, mask):
    bit = 1
    while bit <= mask:
        if mask & bit:
            index = index + bit - 2 * bit * lax.rem(lax.div(index, bit), 2)
        bit *= 2
    return index


def triple(a, b):
    ah, al = halves(a)
    bh, bl = halves(b)
    return nn(ah, bh) + nn(ah, bl) + nn(al, bh)


def fold(x):
    rows = x.shape[0] // 4
    return jnp.concatenate([x[q * rows : (q + 1) * rows] for q in range(4)], axis=1)


def unfold(x):
    width = x.shape[1] // 4
    return jnp.concatenate([x[:, q * width : (q + 1) * width] for q in range(4)], axis=0)


def pair(x):
    rows = x.shape[0] // 2
    return jnp.concatenate([x[:rows], x[rows:]], axis=1)


def unpair(x):
    width = x.shape[1] // 2
    return jnp.concatenate([x[:, :width], x[:, width:]], axis=0)


def kernel(
    panels,
    sub_size,
    order_hbm,
    targets_hbm,
    inverse_hbm,
    basis_hbm,
    coupling_hbm,
    train_hbm,
    test_hbm,
    test_basis_hbm,
    near_hbm,
    out_ref,
    order_ref,
    targets_ref,
    inverse_ref,
    basis_ref,
    coupling_ref,
    train_ref,
    test_ref,
    test_basis_ref,
    near_ref,
    cross_sent,
    cross_received,
    sent,
    received,
    far_sent,
    far_received,
    coord_window,
    features,
    test_features,
    blocks,
    weight_window,
    load_sems,
    leaf_sems,
    cross_send,
    cross_recv,
    round_send,
    round_recv,
    far_send,
    far_recv,
    coord_send,
    coord_recv,
    weight_send,
    weight_recv,
):
    columns, points = targets_ref.shape
    leaf_count, leaf_size = inverse_ref.shape[0], inverse_ref.shape[1]
    levels, rank = basis_ref.shape[0], basis_ref.shape[1]
    near = near_ref.shape[1]
    tests = test_ref.shape[1]
    local = leaf_count.bit_length() - 1
    depth = levels - local
    me = lax.axis_index("leaf") * sub_size + lax.axis_index("sub")

    def load(index, source, target):
        copy = pltpu.make_async_copy(source, target, load_sems.at[index])
        copy.start()
        return copy

    basis_copy = load(0, basis_hbm, basis_ref)
    coupling_copy = load(1, coupling_hbm, coupling_ref)
    order_copy = load(2, order_hbm, order_ref)
    targets_copy = load(3, targets_hbm, targets_ref)
    leaf_copies = []
    for leaf in range(leaf_count):
        copy = pltpu.make_async_copy(
            inverse_hbm.at[leaf], inverse_ref.at[leaf], leaf_sems.at[leaf]
        )
        copy.start()
        leaf_copies.append(copy)
    train_copy = load(4, train_hbm, train_ref)
    test_copy = load(5, test_hbm, test_ref)
    near_copy = load(6, near_hbm, near_ref)
    test_basis_copy = load(7, test_basis_hbm, test_basis_ref)

    def device(index):
        return {"leaf": lax.div(index, sub_size), "sub": lax.rem(index, sub_size)}

    barrier = pltpu.get_barrier_semaphore()
    for mask in range(1, panels):
        pl.semaphore_signal(
            barrier,
            inc=1,
            device_id=device(toggled(me, mask)),
            device_id_type=pl.DeviceIdType.MESH,
        )

    def remote(source, target, send, recv, index):
        return pltpu.make_async_remote_copy(
            src_ref=source,
            dst_ref=target,
            send_sem=send,
            recv_sem=recv,
            device_id=device(index),
            device_id_type=pl.DeviceIdType.MESH,
        )

    def shared(copy_next, copy_prev):
        def start():
            pl.when(me < panels - 1)(copy_next.start)
            pl.when(me > 0)(copy_prev.start)

        def wait():
            pl.when(me < panels - 1)(copy_next.wait_send)
            pl.when(me > 0)(copy_prev.wait_send)
            pl.when(me > 0)(copy_next.wait_recv)
            pl.when(me < panels - 1)(copy_prev.wait_recv)

        return start, wait

    after, before = lax.rem(me + 1, panels), lax.rem(me + panels - 1, panels)

    scale = jnp.concatenate(
        [jnp.full((rank, 1), 1.0 / math.sqrt(leaf_size << level), f32) for level in range(levels)],
        axis=0,
    )
    top = local * rank

    def rows_of(level):
        return slice(level * rank, (level + 1) * rank)

    def first_half(x):
        return x[:, :rank]

    def second_half(x):
        return x[:, rank:]

    basis_copy.wait()
    coupling_copy.wait()
    basis = basis_ref[...].reshape(levels * rank, points)
    coupling = [coupling_ref[0, level] for level in range(levels)]
    bases = [basis[:, leaf * leaf_size : (leaf + 1) * leaf_size] for leaf in range(leaf_count)]
    grams = [nt(one, one) for one in bases]

    def transfer(gram, level):
        below = (level + 1) * rank
        return scale[below:] * triple(gram[below:, rows_of(level)], coupling[level])

    gram = sum(one[top:, top:] for one in grams)
    crossing = []
    for k in range(depth - 1):
        below = (k + 1) * rank
        crossing.append(
            scale[top + below :] * triple(gram[below:, rows_of(k)], coupling[local + k])
        )
    cross_rows = [
        sum((depth - 1 - j) * rank for j in range(b, depth - 1)) // 4 for b in range(depth - 1)
    ]
    cross_starts = [sum(cross_rows[:b]) for b in range(depth - 1)]
    slot_starts = [sum((1 << c) * cross_rows[c] for c in range(b)) for b in range(depth - 1)]
    for b in range(depth - 1):
        parts = [second_half(crossing[b])] + [
            first_half(crossing[j]) for j in range(b + 1, depth - 1)
        ]
        cross_sent[pl.ds(cross_starts[b], cross_rows[b])] = fold(jnp.concatenate(parts, axis=0))

    pl.semaphore_wait(barrier, panels - 1)
    train_copy.wait()
    start_coords, wait_coords = shared(
        remote(train_ref, coord_window.at[0], coord_send.at[0], coord_recv.at[0], after),
        remote(train_ref, coord_window.at[1], coord_send.at[1], coord_recv.at[1], before),
    )
    cross_copies = []
    for b in range(depth - 1):
        for mask in range(1 << b, 2 << b):
            place = slot_starts[b] + (mask - (1 << b)) * cross_rows[b]
            copy = remote(
                cross_sent.at[pl.ds(cross_starts[b], cross_rows[b])],
                cross_received.at[pl.ds(place, cross_rows[b])],
                cross_send.at[mask],
                cross_recv.at[mask],
                toggled(me, mask),
            )
            copy.start()
            cross_copies.append(copy)
    start_coords()

    local_sides = []
    for level in range(local):
        width = 1 << level
        parts = [
            transfer(sum(grams[c * width + i] for i in range(width)), level)
            for c in range(leaf_count // width)
        ]
        local_sides.append(
            [first_half(parts[c]) + second_half(parts[c ^ 1]) for c in range(len(parts))]
        )

    order_copy.wait()
    targets_copy.wait()
    stacked = jnp.concatenate(
        [targets_ref[:, h * CHUNK : (h + 1) * CHUNK] for h in range(points // CHUNK)], axis=0
    )
    order = order_ref[...]
    low, high = lax.rem(order, CHUNK), lax.div(order, CHUNK)
    solved, coefs = [], []
    for leaf in range(leaf_count):
        span = slice(leaf * leaf_size, (leaf + 1) * leaf_size)
        places = lax.broadcasted_iota(jnp.int32, (CHUNK, leaf_size), 0)
        chosen = jnp.where(places == low[:, span], 1.0, 0.0).astype(bf16)
        picked = nn(stacked, chosen)
        taken = jnp.zeros((columns, leaf_size), f32)
        for h in range(points // CHUNK):
            taken = jnp.where(
                high[:, span] == h, picked[h * columns : (h + 1) * columns], taken
            )
        leaf_copies[leaf].wait()
        state = nt(taken.astype(bf16), inverse_ref[leaf])
        state_high, state_low = halves(state)
        coefs.append((nt(bases[leaf], state_high) + nt(bases[leaf], state_low)) * scale)
        solved.append(state)

    mixes = [[] for _ in range(leaf_count)]
    for level in range(local):
        sides = local_sides[level]
        heads = [one[:rank] for one in coefs]
        for leaf in range(leaf_count):
            c = leaf >> level
            if leaf == c << level:
                mixed = triple(
                    coupling[level], jnp.concatenate([heads[c], heads[c ^ 1]], axis=0)
                )
            mixes[leaf].append(mixed)
        coefs = [
            coefs[2 * p][rank:]
            + coefs[2 * p + 1][rank:]
            - triple(sides[2 * p], heads[2 * p])
            - triple(sides[2 * p + 1], heads[2 * p + 1])
            for p in range(len(coefs) // 2)
        ]
    own = coefs[0]

    near_copy.wait()
    test_copy.wait()
    gain = 3.0 / (length_scale * length_scale) * math.log2(math.e) ** 2

    def norm(pos):
        return gain * (pos[0:1] * pos[0:1] + pos[1:2] * pos[1:2] + pos[2:3] * pos[2:3])

    def train_side(pos):
        ones = jnp.ones((3, points), f32)
        zero = jnp.zeros((1, points), f32)
        parts = thirds(-2.0 * gain * pos) + thirds(norm(pos)) + [ones, zero]
        return jnp.concatenate(parts, axis=0).astype(bf16)

    def put_features(panel, pos):
        made = train_side(pos.astype(f32))
        for leaf in range(leaf_count):
            features[panel * leaf_count + leaf] = made[:, leaf * leaf_size : (leaf + 1) * leaf_size]

    first_leaf = (me - 1) * leaf_count

    def window_leaf(slot):
        return jnp.clip(near_ref[0, slot] - first_leaf, 0, 3 * leaf_count - 1)

    def near_block(step, carry):
        slot, tile = lax.div(step, tests // TILE), lax.rem(step, tests // TILE)
        lanes = pl.ds(pl.multiple_of(tile * TILE, TILE), TILE)
        squared = tn(features[window_leaf(slot)], test_features[:, lanes])
        squared = jnp.maximum(squared, 1e-12)
        scaled = squared * lax.rsqrt(squared)
        value = (scaled + 1.0 / math.log(2.0)) * jnp.exp2(
            math.log2(variance * math.log(2.0)) - scaled
        )
        blocks[pl.ds(pl.multiple_of(slot * leaf_size, leaf_size), leaf_size), lanes] = value.astype(
            bf16
        )
        return carry

    total_steps = near * (tests // TILE)
    split = total_steps * EARLY // 16

    for copy in cross_copies:
        copy.wait()
    summed = []
    for b in range(depth - 1):
        total = sum(
            cross_received[pl.ds(slot_starts[b] + i * cross_rows[b], cross_rows[b])]
            for i in range(1 << b)
        )
        flat = unfold(total)
        pieces, place = {}, 0
        for j in range(b, depth - 1):
            size = (depth - 1 - j) * rank
            pieces[j] = flat[place : place + size]
            place += size
        summed.append(pieces)
    rest, flows = own, []
    for j in range(depth):
        flows.append(rest[:rank])
        if j < depth - 1:
            side = first_half(crossing[j]) + sum(summed[b][j] for b in range(j + 1))
            rest = rest[rank:] - triple(side, flows[j])
    for k in range(depth):
        sent[k] = pair(flows[k])
    copies = []
    for mask in range(1, panels):
        b = mask.bit_length() - 1
        copy = remote(
            sent.at[pl.ds(b, depth - b)],
            received.at[mask, pl.ds(b, depth - b)],
            round_send.at[mask],
            round_recv.at[mask],
            toggled(me, mask),
        )
        copy.start()
        copies.append(copy)

    test_pos = test_ref[...].astype(f32)
    ones = jnp.ones((3, tests), f32)
    zero = jnp.zeros((1, tests), f32)
    test_features[...] = jnp.concatenate(
        [test_pos, test_pos, test_pos, ones] + thirds(norm(test_pos)) + [zero], axis=0
    ).astype(bf16)
    put_features(1, train_ref[...])
    wait_coords()
    put_features(0, coord_window[0])
    put_features(2, coord_window[1])
    lax.fori_loop(0, split, near_block, 0)

    for copy in copies:
        copy.wait()
    mixed_far = []
    for k in range(depth):
        mine = flows[k]
        if k:
            mine = mine + unpair(sum(received[mask, k] for mask in range(1, 1 << k)))
        other = unpair(sum(received[mask, k] for mask in range(1 << k, 2 << k)))
        mixed_far.append(triple(coupling[local + k], jnp.concatenate([mine, other], axis=0)))

    terms = jnp.zeros((depth * rank, columns), f32)
    for leaf in range(leaf_count):
        mix = jnp.concatenate(mixes[leaf] + mixed_far, axis=0)
        mix_high, mix_low = halves(mix)
        state = solved[leaf] - tn(mix_high, bases[leaf]) - tn(mix_low, bases[leaf])
        weights = state.astype(bf16)
        weight_window[leaf_count + leaf] = weights
        terms = terms + nt(bases[leaf][top:], weights)
    panel = weight_window.at[pl.ds(leaf_count, leaf_count)]
    start_weights, wait_weights = shared(
        remote(
            panel,
            weight_window.at[pl.ds(0, leaf_count)],
            weight_send.at[0],
            weight_recv.at[0],
            after,
        ),
        remote(
            panel,
            weight_window.at[pl.ds(2 * leaf_count, leaf_count)],
            weight_send.at[1],
            weight_recv.at[1],
            before,
        ),
    )
    start_weights()
    terms = terms * scale[top:]
    for k in range(depth):
        far_sent[k] = pair(terms[rows_of(k)])
    far_copies = []
    for mask in range(1, panels):
        copy = remote(
            far_sent.at[mask.bit_length() - 1],
            far_received.at[mask],
            far_send.at[mask],
            far_recv.at[mask],
            toggled(me, mask),
        )
        copy.start()
        far_copies.append(copy)
    lax.fori_loop(split, total_steps, near_block, 0)
    for copy in far_copies:
        copy.wait()
    far_rows = []
    for k in range(depth):
        far_rows.append(unpair(sum(far_received[mask] for mask in range(1 << k, 2 << k))))
    far_high, far_low = halves(jnp.concatenate(far_rows, axis=0))
    test_basis_copy.wait()
    test_basis = test_basis_ref[...].reshape(depth * rank, tests)
    wait_weights()
    held = jnp.concatenate(
        [weight_window[window_leaf(slot)] for slot in range(near)], axis=1
    )
    for tile in range(tests // TILE):
        lanes = slice(tile * TILE, (tile + 1) * TILE)
        near_sum = nn(held, blocks[:, lanes])
        far_sum = tn(far_high, test_basis[:, lanes]) + tn(far_low, test_basis[:, lanes])
        out_ref[:, lanes] = (near_sum * (1.0 / math.sqrt(near * leaf_size)) + far_sum).astype(bf16)


def shards(
    panels,
    sub_size,
    targets,
    tree_order,
    leaf_inverse,
    cluster_basis,
    coupling,
    train_coords,
    test_coords,
    test_basis,
    near_leaves,
):
    columns, points = targets.shape
    leaf_count, leaf_size = leaf_inverse.shape[0], leaf_inverse.shape[1]
    levels, rank = cluster_basis.shape[0], cluster_basis.shape[1]
    near = near_leaves.shape[1]
    tests = test_coords.shape[1]
    depth = levels - (leaf_count.bit_length() - 1)
    cross_rows = [
        sum((depth - 1 - j) * rank for j in range(b, depth - 1)) // 4 for b in range(depth - 1)
    ]
    slots = sum((1 << b) * cross_rows[b] for b in range(depth - 1))
    vmem = pl.BlockSpec(memory_space=pltpu.VMEM)
    anywhere = pl.BlockSpec(memory_space=pl.ANY)
    sems = pltpu.SemaphoreType.DMA
    operands = (
        tree_order,
        targets,
        leaf_inverse,
        cluster_basis,
        coupling,
        train_coords,
        test_coords,
        test_basis,
    )
    return pl.pallas_call(
        functools.partial(kernel, panels, sub_size),
        out_shape=jax.ShapeDtypeStruct((columns, tests), bf16),
        in_specs=[anywhere] * 9,
        out_specs=vmem,
        scratch_shapes=[pltpu.VMEM(one.shape, one.dtype) for one in operands]
        + [
            pltpu.SMEM(near_leaves.shape, near_leaves.dtype),
            pltpu.VMEM((sum(cross_rows), 4 * rank), f32),
            pltpu.VMEM((slots, 4 * rank), f32),
            pltpu.VMEM((depth, rank // 2, 2 * columns), f32),
            pltpu.VMEM((panels, depth, rank // 2, 2 * columns), f32),
            pltpu.VMEM((depth, rank // 2, 2 * columns), f32),
            pltpu.VMEM((panels, rank // 2, 2 * columns), f32),
            pltpu.VMEM((2, 3, points), bf16),
            pltpu.VMEM((3 * leaf_count, FEATS, leaf_size), bf16),
            pltpu.VMEM((FEATS, tests), bf16),
            pltpu.VMEM((near * leaf_size, tests), bf16),
            pltpu.VMEM((3 * leaf_count, columns, leaf_size), bf16),
            sems((8,)),
            sems((leaf_count,)),
            sems((panels,)),
            sems((panels,)),
            sems((panels,)),
            sems((panels,)),
            sems((panels,)),
            sems((panels,)),
            sems((2,)),
            sems((2,)),
            sems((2,)),
            sems((2,)),
        ],
        compiler_params=pltpu.CompilerParams(
            collective_id=0, has_side_effects=True, vmem_limit_bytes=60 * 1024 * 1024
        ),
    )(*operands, near_leaves)


def solution(mesh):
    return jax.shard_map(
        functools.partial(shards, mesh.shape["leaf"] * mesh.shape["sub"], mesh.shape["sub"]),
        mesh=mesh,
        in_specs=(
            P(None, ("grp", "leaf", "sub")),
            P(("grp", "leaf", "sub"), None),
            P(("grp", "leaf", "sub"), None, None),
            P(None, None, ("grp", "leaf", "sub")),
            P(("grp", "leaf", "sub"), None, None, None),
            P(None, ("grp", "leaf", "sub")),
            P(None, ("grp", "leaf", "sub")),
            P(None, None, ("grp", "leaf", "sub")),
            P(("grp", "leaf", "sub"), None),
        ),
        out_specs=P(None, ("grp", "leaf", "sub")),
        check_vma=False,
    )
```

time: 35.6 us -> 32.4 us (0.910)
  Pallas kernels: 33.8 us -> 30.6 us
    pallas_call x1, Pallas kernels: 33.8 us -> 30.6 us  [shards(): pl.pallas_call(functools.partial(kernel, panels, sub_size), out_shape=jax...]
where the time goes in v1:
time: 32.4 us; the launch traced here: 32.3 us
  Pallas kernels  30.6 us (94%)
  local copies, waits for them, and re-layouts  1.67 us (5%)
    pallas_call x1, Pallas kernels, shards(): pl.pallas_call(functools.partial(kernel, panels, sub_size), out_shape=jax...  30.6 us
    unnamed x1, local copies, waits for them, and re-layouts  1.67 us

profile of v1, /device:TPU:0, one launch (start us, length us, event | category | flops | bytes accessed | tf_op | source)
XLA Modules:
  0.0 32.3 jit_solution(13729644788597733711)
XLA Ops:
  0.0 30.6 %shard_map.91 = bf16[64,2048]{1,0:T(8,128)(2,1)} custom-call(s32[1,2048]{1,0:T(1,128)} %order_hbm.1, bf16[64,2048]{1,0:T(8,128)(2,1)} %targets_hbm.1, bf16[4,512,512]{2,1,0:T(8,128)(2,1)} %inverse_hbm.1, bf16[6,32,2048]{2,1,0:T(8,128)(2,1)} %basis_hbm.1, f32[1,6,32,64]{3,2,1,0:T(8,128)} %coupling_hbm.1, bf16[3,2048]{1,0:T(4,128)(2,1)} %train_hbm.1, ...), custom_call_target="tpu_custom_call" | custom-call | tf_op jit(solution)/shard_map/pallas_call | solution.py:506
  30.6 1.7 %copy.11 = bf16[64,2048]{1,0:T(8,128)(2,1)} copy(bf16[64,2048]{1,0:T(8,128)(2,1)} %shard_map.91) | data formatting | bytes 524288

commit v2 on v1

v2 whole, which is shorter than its diff:
```python
import functools
import math

import jax
import jax.numpy as jnp
from jax import lax
from jax.experimental import pallas as pl
from jax.experimental.pallas import tpu as pltpu
from jax.sharding import PartitionSpec as P

variance = 2.0
length_scale = 0.5
f32 = jnp.float32
bf16 = jnp.bfloat16
CHUNK = 256
TILE = 1024
FEATS = 16
EARLY = 4
FIRST = 5
GUARD = 2.0**-12


def nt(a, b):
    return lax.dot_general(a, b, (((1,), (1,)), ((), ())), preferred_element_type=f32)


def nn(a, b):
    return jnp.dot(a, b, preferred_element_type=f32)


def tn(a, b):
    return lax.dot_general(a, b, (((0,), (0,)), ((), ())), preferred_element_type=f32)


def halves(x):
    high = x.astype(bf16)
    return high, (x - high.astype(f32)).astype(bf16)


def thirds(x):
    first = x.astype(bf16).astype(f32)
    second = (x - first).astype(bf16).astype(f32)
    return [first, second, (x - first - second).astype(bf16).astype(f32)]


def toggled(index, mask):
    bit = 1
    while bit <= mask:
        if mask & bit:
            index = index + bit - 2 * bit * lax.rem(lax.div(index, bit), 2)
        bit *= 2
    return index


def triple(a, b):
    ah, al = halves(a)
    bh, bl = halves(b)
    return nn(ah, bh) + nn(ah, bl) + nn(al, bh)


def fold(x):
    rows = x.shape[0] // 4
    return jnp.concatenate([x[q * rows : (q + 1) * rows] for q in range(4)], axis=1)


def unfold(x):
    width = x.shape[1] // 4
    return jnp.concatenate([x[:, q * width : (q + 1) * width] for q in range(4)], axis=0)


def pair(x):
    rows = x.shape[0] // 2
    return jnp.concatenate([x[:rows], x[rows:]], axis=1)


def unpair(x):
    width = x.shape[1] // 2
    return jnp.concatenate([x[:, :width], x[:, width:]], axis=0)


def spans(depth, rank, parts):
    cross = [sum((depth - 1 - j) * rank for j in range(b, depth - 1)) // 4 for b in range(depth)]
    upper = [(depth - b) * rank // 2 for b in range(depth)]
    rows = cross if parts == "cross" else upper
    starts = [sum(rows[:b]) for b in range(depth + 1)]
    slots = [sum((1 << c) * rows[c] for c in range(b)) for b in range(depth + 1)]
    return rows, starts, slots


def kernel(
    panels,
    sub_size,
    order_hbm,
    targets_hbm,
    inverse_hbm,
    basis_hbm,
    coupling_hbm,
    train_hbm,
    test_hbm,
    test_basis_hbm,
    near_hbm,
    out_hbm,
    order_ref,
    targets_ref,
    inverse_ref,
    basis_ref,
    coupling_ref,
    train_ref,
    test_ref,
    test_basis_ref,
    near_ref,
    out_ref,
    cross_sent,
    cross_received,
    upper_sent,
    upper_received,
    sent,
    received,
    coord_window,
    features,
    test_features,
    blocks,
    pair_weights,
    side_weights,
    held,
    total,
    load_sems,
    leaf_sems,
    out_sems,
    cross_send,
    cross_recv,
    upper_send,
    upper_recv,
    round_send,
    round_recv,
    coord_send,
    coord_recv,
    pair_send,
    pair_recv,
    side_send,
    side_recv,
):
    columns, points = targets_ref.shape
    leaf_count, leaf_size = inverse_ref.shape[0], inverse_ref.shape[1]
    levels, rank = basis_ref.shape[0], basis_ref.shape[1]
    near = near_ref.shape[1]
    tests = test_ref.shape[1]
    local = leaf_count.bit_length() - 1
    depth = levels - local
    half = panels // 2
    me = lax.axis_index("leaf") * sub_size + lax.axis_index("sub")

    def load(index, source, target):
        copy = pltpu.make_async_copy(source, target, load_sems.at[index])
        copy.start()
        return copy

    basis_copy = load(0, basis_hbm, basis_ref)
    coupling_copy = load(1, coupling_hbm, coupling_ref)
    order_copy = load(2, order_hbm, order_ref)
    targets_copy = load(3, targets_hbm, targets_ref)
    leaf_copies = []
    for leaf in range(leaf_count):
        copy = pltpu.make_async_copy(
            inverse_hbm.at[leaf], inverse_ref.at[leaf], leaf_sems.at[leaf]
        )
        copy.start()
        leaf_copies.append(copy)
    train_copy = load(4, train_hbm, train_ref)
    test_copy = load(5, test_hbm, test_ref)
    near_copy = load(6, near_hbm, near_ref)
    test_basis_copy = load(7, test_basis_hbm, test_basis_ref)

    def device(index):
        return {"leaf": lax.div(index, sub_size), "sub": lax.rem(index, sub_size)}

    odd = lax.rem(me, 2)
    mate = me + 1 - 2 * odd
    side = me - 1 + 2 * odd
    has_side = (side >= 0) & (side < panels)
    side_safe = jnp.clip(side, 0, panels - 1)
    middle = (me == half - 1) | (me == half)
    greeted = list(range(1, half)) + [half]

    barrier = pltpu.get_barrier_semaphore()

    def greet(index):
        pl.semaphore_signal(
            barrier, inc=1, device_id=device(index), device_id_type=pl.DeviceIdType.MESH
        )

    @pl.when(jnp.logical_not(has_side))
    def _():
        side_weights[...] = jnp.zeros_like(side_weights)

    for mask in greeted:
        greet(toggled(me, mask))
    if panels > 2:
        pl.when(middle)(lambda: greet(side_safe))

    def remote(source, target, send, recv, index):
        return pltpu.make_async_remote_copy(
            src_ref=source,
            dst_ref=target,
            send_sem=send,
            recv_sem=recv,
            device_id=device(index),
            device_id_type=pl.DeviceIdType.MESH,
        )

    scale = jnp.concatenate(
        [jnp.full((rank, 1), 1.0 / math.sqrt(leaf_size << level), f32) for level in range(levels)],
        axis=0,
    )
    top = local * rank

    def rows_of(level):
        return slice(level * rank, (level + 1) * rank)

    def first_half(x):
        return x[:, :rank]

    def second_half(x):
        return x[:, rank:]

    basis_copy.wait()
    coupling_copy.wait()
    basis = basis_ref[...].reshape(levels * rank, points)
    coupling = [coupling_ref[0, level] for level in range(levels)]
    bases = [basis[:, leaf * leaf_size : (leaf + 1) * leaf_size] for leaf in range(leaf_count)]
    grams = [nt(one, one) for one in bases]
    gram = sum(one[top:, top:] for one in grams)
    moved = [
        scale[top:] * triple(gram[:, rows_of(k)], coupling[local + k]) for k in range(depth)
    ]
    crossing = [moved[k][(k + 1) * rank :] for k in range(depth - 1)]
    cross_rows, cross_starts, cross_slots = spans(depth, rank, "cross")
    upper_rows, upper_starts, upper_slots = spans(depth, rank, "upper")
    for b in range(depth - 1):
        parts = [second_half(crossing[b])] + [
            first_half(crossing[j]) for j in range(b + 1, depth - 1)
        ]
        cross_sent[pl.ds(cross_starts[b], cross_rows[b])] = fold(jnp.concatenate(parts, axis=0))

    def spread(b, mask, source, target, rows, starts, slots, send, recv):
        place = slots[b] + (mask - (1 << b)) * rows[b]
        copy = remote(
            source.at[pl.ds(starts[b], rows[b])],
            target.at[pl.ds(place, rows[b])],
            send.at[mask],
            recv.at[mask],
            toggled(me, mask),
        )
        copy.start()
        return copy

    def spread_upper(b, mask):
        return spread(
            b,
            mask,
            upper_sent,
            upper_received,
            upper_rows,
            upper_starts,
            upper_slots,
            upper_send,
            upper_recv,
        )

    extra = middle.astype(jnp.int32) if panels > 2 else 0
    pl.semaphore_wait(barrier, len(greeted) + extra)
    cross_copies, upper_copies = [], []
    for b in range(depth - 1):
        for mask in range(1 << b, 2 << b):
            cross_copies.append(
                spread(
                    b,
                    mask,
                    cross_sent,
                    cross_received,
                    cross_rows,
                    cross_starts,
                    cross_slots,
                    cross_send,
                    cross_recv,
                )
            )
    train_copy.wait()
    mate_coords = remote(train_ref, coord_window.at[0], coord_send.at[0], coord_recv.at[0], mate)
    side_coords = remote(
        train_ref, coord_window.at[1], coord_send.at[1], coord_recv.at[1], side_safe
    )
    mate_coords.start()
    pl.when(has_side)(side_coords.start)

    def transfer(gram, level):
        below = (level + 1) * rank
        return scale[below:] * triple(gram[below:, rows_of(level)], coupling[level])

    local_sides = []
    for level in range(local):
        width = 1 << level
        parts = [
            transfer(sum(grams[c * width + i] for i in range(width)), level)
            for c in range(leaf_count // width)
        ]
        local_sides.append(
            [first_half(parts[c]) + second_half(parts[c ^ 1]) for c in range(len(parts))]
        )

    order_copy.wait()
    targets_copy.wait()
    for copy in leaf_copies:
        copy.wait()
    near_copy.wait()
    test_copy.wait()
    stacked = jnp.concatenate(
        [targets_ref[:, h * CHUNK : (h + 1) * CHUNK] for h in range(points // CHUNK)], axis=0
    )
    order = order_ref[...]
    low, high = lax.rem(order, CHUNK), lax.div(order, CHUNK)
    solved, coefs = [], []
    for leaf in range(leaf_count):
        span = slice(leaf * leaf_size, (leaf + 1) * leaf_size)
        places = lax.broadcasted_iota(jnp.int32, (CHUNK, leaf_size), 0)
        chosen = jnp.where(places == low[:, span], 1.0, 0.0).astype(bf16)
        picked = nn(stacked, chosen)
        taken = jnp.zeros((columns, leaf_size), f32)
        for h in range(points // CHUNK):
            taken = jnp.where(
                high[:, span] == h, picked[h * columns : (h + 1) * columns], taken
            )
        state = nt(taken.astype(bf16), inverse_ref[leaf])
        state_high, state_low = halves(state)
        coefs.append((nt(bases[leaf], state_high) + nt(bases[leaf], state_low)) * scale)
        solved.append(state)

    mixes = [[] for _ in range(leaf_count)]
    for level in range(local):
        sides = local_sides[level]
        heads = [one[:rank] for one in coefs]
        for leaf in range(leaf_count):
            c = leaf >> level
            if leaf == c << level:
                mixed = triple(
                    coupling[level], jnp.concatenate([heads[c], heads[c ^ 1]], axis=0)
                )
            mixes[leaf].append(mixed)
        coefs = [
            coefs[2 * p][rank:]
            + coefs[2 * p + 1][rank:]
            - triple(sides[2 * p], heads[2 * p])
            - triple(sides[2 * p + 1], heads[2 * p + 1])
            for p in range(len(coefs) // 2)
        ]
    own = coefs[0]

    for copy in cross_copies:
        copy.wait()
    summed = []
    for b in range(depth - 1):
        flat = unfold(
            sum(
                cross_received[pl.ds(cross_slots[b] + i * cross_rows[b], cross_rows[b])]
                for i in range(1 << b)
            )
        )
        pieces, place = {}, 0
        for j in range(b, depth - 1):
            size = (depth - 1 - j) * rank
            pieces[j] = flat[place : place + size]
            place += size
        summed.append(pieces)
    rest, flows = own, []
    for j in range(depth):
        flows.append(rest[:rank])
        if j < depth - 1:
            side_sum = first_half(crossing[j]) + sum(summed[b][j] for b in range(j + 1))
            rest = rest[rank:] - triple(side_sum, flows[j])
    for k in range(depth):
        sent[k] = pair(flows[k]).astype(bf16)
    copies = []
    for mask in reversed(range(1, panels)):
        b = mask.bit_length() - 1
        copy = remote(
            sent.at[pl.ds(b, depth - b)],
            received.at[mask, pl.ds(b, depth - b)],
            round_send.at[mask],
            round_recv.at[mask],
            toggled(me, mask),
        )
        copy.start()
        copies.append(copy)
    for b in range(depth):
        parts = [moved[j][rows_of(b)] for j in range(b, depth)]
        upper_sent[pl.ds(upper_starts[b], upper_rows[b])] = pair(jnp.concatenate(parts, axis=0))
    for b in range(depth):
        for mask in range(1 << b, 2 << b):
            upper_copies.append(spread_upper(b, mask))

    gain = 3.0 / (length_scale * length_scale) * math.log2(math.e) ** 2

    def norm(pos):
        return gain * (pos[0:1] * pos[0:1] + pos[1:2] * pos[1:2] + pos[2:3] * pos[2:3])

    def train_side(pos):
        ones = jnp.ones((3, points), f32)
        zero = jnp.zeros((1, points), f32)
        parts = thirds(-2.0 * gain * pos) + thirds(norm(pos)) + [ones, zero + GUARD]
        return jnp.concatenate(parts, axis=0).astype(bf16)

    def put_features(panel, pos):
        made = train_side(pos.astype(f32))
        for leaf in range(leaf_count):
            features[panel * leaf_count + leaf] = made[:, leaf * leaf_size : (leaf + 1) * leaf_size]

    test_pos = test_ref[...].astype(f32)
    ones = jnp.ones((3, tests), f32)
    zero = jnp.zeros((1, tests), f32)
    test_features[...] = jnp.concatenate(
        [test_pos, test_pos, test_pos, ones] + thirds(norm(test_pos)) + [zero + 1.0], axis=0
    ).astype(bf16)
    put_features(0, train_ref[...])
    for leaf in range(leaf_count):
        mix_high, mix_low = halves(jnp.concatenate(mixes[leaf], axis=0))
        solved[leaf] = (
            solved[leaf] - tn(mix_high, bases[leaf][:top]) - tn(mix_low, bases[leaf][:top])
        )

    def within(place):
        return jnp.clip(place + 1, 0, 1) * jnp.clip(leaf_count - place, 0, 1)

    def window_leaf(slot):
        leaf_id = near_ref[0, slot]
        in_own = leaf_id - me * leaf_count
        in_mate = leaf_id - mate * leaf_count
        in_side = jnp.clip(leaf_id - side * leaf_count, 0, leaf_count - 1)
        is_own, is_mate = within(in_own), within(in_mate)
        return (
            is_own * in_own
            + is_mate * (leaf_count + in_mate)
            + (1 - is_own - is_mate) * (2 * leaf_count + in_side)
        )

    def kept(weights, flag):
        return (weights.astype(f32) * flag.astype(f32)).astype(bf16)

    tiles = tests // TILE

    def near_block(slot, carry):
        squared = tn(features[window_leaf(slot)], test_features[...])
        scaled = squared * lax.rsqrt(squared)
        value = (scaled + 1.0 / math.log(2.0)) * jnp.exp2(
            math.log2(variance * math.log(2.0)) - scaled
        )
        blocks[slot] = value.astype(bf16)
        return carry

    def add_block(slot):
        total[...] = total[...] + nn(held[slot], blocks[slot])

    early = near * EARLY // 8
    first = near * FIRST // 8

    mate_coords.wait()
    put_features(1, coord_window[0])
    pl.when(has_side)(side_coords.wait)
    put_features(2, coord_window[1])
    lax.fori_loop(0, early, near_block, 0)

    for copy in copies:
        copy.wait()
    mines, others, mixed_far = [], [], []
    for k in range(depth):
        mine = flows[k]
        if k:
            mine = mine + unpair(sum(received[mask, k].astype(f32) for mask in range(1, 1 << k)))
        other = unpair(sum(received[mask, k].astype(f32) for mask in range(1 << k, 2 << k)))
        mines.append(mine)
        others.append(other)
        mixed_far.append(triple(coupling[local + k], jnp.concatenate([mine, other], axis=0)))

    far_mix_high, far_mix_low = halves(jnp.concatenate(mixed_far, axis=0))
    side_copies = []
    for leaf in range(leaf_count):
        upper_basis = bases[leaf][top:]
        state = solved[leaf] - tn(far_mix_high, upper_basis) - tn(far_mix_low, upper_basis)
        pair_weights[leaf] = state.astype(bf16)
        copy = remote(
            pair_weights.at[leaf],
            side_weights.at[leaf],
            side_send.at[leaf],
            side_recv.at[leaf],
            side_safe,
        )
        pl.when(has_side)(copy.start)
        side_copies.append(copy)
    mate_weights = remote(
        pair_weights.at[pl.ds(0, leaf_count)],
        pair_weights.at[pl.ds(leaf_count, leaf_count)],
        pair_send.at[0],
        pair_recv.at[0],
        mate,
    )
    mate_weights.start()

    lax.fori_loop(early, first, near_block, 0)
    for copy in upper_copies:
        copy.wait()
    far_rows = []
    for b in range(depth):
        flat = unpair(
            sum(
                upper_received[pl.ds(upper_slots[b] + i * upper_rows[b], upper_rows[b])]
                for i in range(1 << b)
            )
        )
        row = others[b]
        for j in range(b, depth):
            joined = [others[j], mines[j]] if j == b else [mines[j], others[j]]
            row = row - triple(flat[rows_of(j - b)], jnp.concatenate(joined, axis=0))
        far_rows.append(row)
    far_high, far_low = halves(jnp.concatenate(far_rows, axis=0))
    test_basis_copy.wait()
    test_basis = test_basis_ref[...].reshape(depth * rank, tests)
    weigh = math.sqrt(near * leaf_size)
    for tile in range(tiles):
        lanes = slice(tile * TILE, (tile + 1) * TILE)
        total[:, lanes] = weigh * (
            tn(far_high, test_basis[:, lanes]) + tn(far_low, test_basis[:, lanes])
        )
    mate_weights.wait()
    for slot in range(near):
        index = window_leaf(slot)
        weights = pair_weights[jnp.minimum(index, 2 * leaf_count - 1)]
        held[slot] = kept(weights, jnp.clip(2 * leaf_count - index, 0, 1))

    added = 0
    for slot in range(first, near):
        upto = max(min(added + 2, slot), 0)
        for done in range(added, upto):
            add_block(done)
        added = upto
        near_block(slot, 0)
    for slot in range(added, near):
        add_block(slot)

    places, arrived = [], []
    for leaf in range(leaf_count):
        pl.when(has_side)(side_copies[leaf].wait)
    for leaf in range(leaf_count):
        found, where = 0, 0
        for slot in range(near):
            away = window_leaf(slot) - 2 * leaf_count - leaf
            match = jnp.clip(1 - away * away, 0, 1)
            found = found + match
            where = where + match * slot
        arrived.append(kept(side_weights[leaf], jnp.clip(found, 0, 1)))
        places.append(jnp.clip(where, 0, near - 1))
    out_copies = []
    for tile in range(tiles):
        lanes = slice(tile * TILE, (tile + 1) * TILE)
        value = total[:, lanes]
        for weights, where in zip(arrived, places):
            value = value + nn(weights, blocks[where, :, lanes])
        out_ref[:, lanes] = (value * (1.0 / weigh)).astype(bf16)
        copy = pltpu.make_async_copy(out_ref.at[:, lanes], out_hbm.at[:, lanes], out_sems.at[tile])
        copy.start()
        out_copies.append(copy)
    for copy in out_copies:
        copy.wait()


def shards(
    panels,
    sub_size,
    targets,
    tree_order,
    leaf_inverse,
    cluster_basis,
    coupling,
    train_coords,
    test_coords,
    test_basis,
    near_leaves,
):
    columns, points = targets.shape
    leaf_count, leaf_size = leaf_inverse.shape[0], leaf_inverse.shape[1]
    levels, rank = cluster_basis.shape[0], cluster_basis.shape[1]
    near = near_leaves.shape[1]
    tests = test_coords.shape[1]
    depth = levels - (leaf_count.bit_length() - 1)
    cross_starts, cross_slots = spans(depth, rank, "cross")[1:]
    upper_starts, upper_slots = spans(depth, rank, "upper")[1:]
    anywhere = pl.BlockSpec(memory_space=pl.ANY)
    sems = pltpu.SemaphoreType.DMA
    operands = (
        tree_order,
        targets,
        leaf_inverse,
        cluster_basis,
        coupling,
        train_coords,
        test_coords,
        test_basis,
    )
    return pl.pallas_call(
        functools.partial(kernel, panels, sub_size),
        out_shape=jax.ShapeDtypeStruct((columns, tests), bf16),
        in_specs=[anywhere] * 9,
        out_specs=anywhere,
        scratch_shapes=[pltpu.VMEM(one.shape, one.dtype) for one in operands]
        + [
            pltpu.SMEM(near_leaves.shape, near_leaves.dtype),
            pltpu.VMEM((columns, tests), bf16),
            pltpu.VMEM((cross_starts[-1], 4 * rank), f32),
            pltpu.VMEM((cross_slots[-1], 4 * rank), f32),
            pltpu.VMEM((upper_starts[-1], 4 * rank), f32),
            pltpu.VMEM((upper_slots[-1], 4 * rank), f32),
            pltpu.VMEM((depth, rank // 2, 2 * columns), bf16),
            pltpu.VMEM((panels, depth, rank // 2, 2 * columns), bf16),
            pltpu.VMEM((2, 3, points), bf16),
            pltpu.VMEM((3 * leaf_count, FEATS, leaf_size), bf16),
            pltpu.VMEM((FEATS, tests), bf16),
            pltpu.VMEM((near, leaf_size, tests), bf16),
            pltpu.VMEM((2 * leaf_count, columns, leaf_size), bf16),
            pltpu.VMEM((leaf_count, columns, leaf_size), bf16),
            pltpu.VMEM((near, columns, leaf_size), bf16),
            pltpu.VMEM((columns, tests), f32),
            sems((8,)),
            sems((leaf_count,)),
            sems((tests // TILE,)),
            sems((panels,)),
            sems((panels,)),
            sems((panels,)),
            sems((panels,)),
            sems((panels,)),
            sems((panels,)),
            sems((2,)),
            sems((2,)),
            sems((1,)),
            sems((1,)),
            sems((leaf_count,)),
            sems((leaf_count,)),
        ],
        compiler_params=pltpu.CompilerParams(
            collective_id=0, has_side_effects=True, vmem_limit_bytes=60 * 1024 * 1024
        ),
    )(*operands, near_leaves)


def solution(mesh):
    return jax.shard_map(
        functools.partial(shards, mesh.shape["leaf"] * mesh.shape["sub"], mesh.shape["sub"]),
        mesh=mesh,
        in_specs=(
            P(None, ("grp", "leaf", "sub")),
            P(("grp", "leaf", "sub"), None),
            P(("grp", "leaf", "sub"), None, None),
            P(None, None, ("grp", "leaf", "sub")),
            P(("grp", "leaf", "sub"), None, None, None),
            P(None, ("grp", "leaf", "sub")),
            P(None, ("grp", "leaf", "sub")),
            P(None, None, ("grp", "leaf", "sub")),
            P(("grp", "leaf", "sub"), None),
        ),
        out_specs=P(None, ("grp", "leaf", "sub")),
        check_vma=False,
    )
```

time: 32.4 us -> 28.7 us (0.89)
  Pallas kernels: 30.6 us -> 26.9 us
    pallas_call x1, Pallas kernels: 30.6 us -> 26.9 us  [shards(): pl.pallas_call(functools.partial(kernel, panels, sub_size), out_shape=jax...]
where the time goes in v2:
time: 28.7 us; the launch traced here: 28.5 us
  Pallas kernels  26.9 us (94%)
  local copies, waits for them, and re-layouts  1.67 us (6%)
    pallas_call x1, Pallas kernels, shards(): pl.pallas_call(functools.partial(kernel, panels, sub_size), out_shape=jax...  26.9 us
    unnamed x1, local copies, waits for them, and re-layouts  1.67 us

profile of v2, /device:TPU:0, one launch (start us, length us, event | category | flops | bytes accessed | tf_op | source)
XLA Modules:
  0.0 28.5 jit_solution(16207907247307218172)
XLA Ops:
  0.0 26.9 %shard_map.91 = bf16[64,2048]{1,0:T(8,128)(2,1)} custom-call(s32[1,2048]{1,0:T(1,128)} %order_hbm.1, bf16[64,2048]{1,0:T(8,128)(2,1)} %targets_hbm.1, bf16[4,512,512]{2,1,0:T(8,128)(2,1)} %inverse_hbm.1, bf16[6,32,2048]{2,1,0:T(8,128)(2,1)} %basis_hbm.1, f32[1,6,32,64]{3,2,1,0:T(8,128)} %coupling_hbm.1, bf16[3,2048]{1,0:T(4,128)(2,1)} %train_hbm.1, ...), custom_call_target="tpu_custom_call" | custom-call | tf_op jit(solution)/shard_map/pallas_call | solution.py:607
  26.9 1.7 %copy.11 = bf16[64,2048]{1,0:T(8,128)(2,1)} copy(bf16[64,2048]{1,0:T(8,128)(2,1)} %shard_map.91) | data formatting | bytes 524288

commit v3 on v2

--- a/solution.py
+++ b/solution.py
@@ -16,7 +16,7 @@
 TILE = 1024
 FEATS = 16
 EARLY = 4
-FIRST = 5
+MIDDLE = 7
 GUARD = 2.0**-12
 
 
@@ -120,12 +120,8 @@
     features,
     test_features,
     blocks,
-    pair_weights,
-    side_weights,
-    held,
-    total,
+    weight_window,
     load_sems,
-    leaf_sems,
     out_sems,
     cross_send,
     cross_recv,
@@ -159,13 +155,7 @@
     coupling_copy = load(1, coupling_hbm, coupling_ref)
     order_copy = load(2, order_hbm, order_ref)
     targets_copy = load(3, targets_hbm, targets_ref)
-    leaf_copies = []
-    for leaf in range(leaf_count):
-        copy = pltpu.make_async_copy(
-            inverse_hbm.at[leaf], inverse_ref.at[leaf], leaf_sems.at[leaf]
-        )
-        copy.start()
-        leaf_copies.append(copy)
+    inverse_copy = load(8, inverse_hbm, inverse_ref)
     train_copy = load(4, train_hbm, train_ref)
     test_copy = load(5, test_hbm, test_ref)
     near_copy = load(6, near_hbm, near_ref)
@@ -188,10 +178,6 @@
         pl.semaphore_signal(
             barrier, inc=1, device_id=device(index), device_id_type=pl.DeviceIdType.MESH
         )
-
-    @pl.when(jnp.logical_not(has_side))
-    def _():
-        side_weights[...] = jnp.zeros_like(side_weights)
 
     for mask in greeted:
         greet(toggled(me, mask))
@@ -244,18 +230,16 @@
 
     def spread(b, mask, source, target, rows, starts, slots, send, recv):
         place = slots[b] + (mask - (1 << b)) * rows[b]
-        copy = remote(
+        remote(
             source.at[pl.ds(starts[b], rows[b])],
             target.at[pl.ds(place, rows[b])],
-            send.at[mask],
-            recv.at[mask],
+            send.at[0],
+            recv.at[0],
             toggled(me, mask),
-        )
-        copy.start()
-        return copy
+        ).start()
 
     def spread_upper(b, mask):
-        return spread(
+        spread(
             b,
             mask,
             upper_sent,
@@ -269,21 +253,18 @@
 
     extra = middle.astype(jnp.int32) if panels > 2 else 0
     pl.semaphore_wait(barrier, len(greeted) + extra)
-    cross_copies, upper_copies = [], []
     for b in range(depth - 1):
         for mask in range(1 << b, 2 << b):
-            cross_copies.append(
-                spread(
-                    b,
-                    mask,
-                    cross_sent,
-                    cross_received,
-                    cross_rows,
-                    cross_starts,
-                    cross_slots,
-                    cross_send,
-                    cross_recv,
-                )
+            spread(
+                b,
+                mask,
+                cross_sent,
+                cross_received,
+                cross_rows,
+                cross_starts,
+                cross_slots,
+                cross_send,
+                cross_recv,
             )
     train_copy.wait()
     mate_coords = remote(train_ref, coord_window.at[0], coord_send.at[0], coord_recv.at[0], mate)
@@ -310,8 +291,7 @@
 
     order_copy.wait()
     targets_copy.wait()
-    for copy in leaf_copies:
-        copy.wait()
+    inverse_copy.wait()
     near_copy.wait()
     test_copy.wait()
     stacked = jnp.concatenate(
@@ -355,8 +335,7 @@
         ]
     own = coefs[0]
 
-    for copy in cross_copies:
-        copy.wait()
+    remote(cross_received, cross_received, cross_send.at[0], cross_recv.at[0], mate).wait()
     summed = []
     for b in range(depth - 1):
         flat = unfold(
@@ -378,25 +357,28 @@
             side_sum = first_half(crossing[j]) + sum(summed[b][j] for b in range(j + 1))
             rest = rest[rank:] - triple(side_sum, flows[j])
     for k in range(depth):
-        sent[k] = pair(flows[k]).astype(bf16)
-    copies = []
+        sent[k] = pair(flows[k])
+    unit_starts, units = [0], 0
+    for mask in range(1, panels):
+        unit_starts.append(units)
+        units += depth - (mask.bit_length() - 1)
     for mask in reversed(range(1, panels)):
         b = mask.bit_length() - 1
-        copy = remote(
+        remote(
             sent.at[pl.ds(b, depth - b)],
-            received.at[mask, pl.ds(b, depth - b)],
-            round_send.at[mask],
-            round_recv.at[mask],
+            received.at[pl.ds(unit_starts[mask], depth - b)],
+            round_send.at[0],
+            round_recv.at[0],
             toggled(me, mask),
-        )
-        copy.start()
-        copies.append(copy)
+        ).start()
     for b in range(depth):
         parts = [moved[j][rows_of(b)] for j in range(b, depth)]
-        upper_sent[pl.ds(upper_starts[b], upper_rows[b])] = pair(jnp.concatenate(parts, axis=0))
+        upper_sent[pl.ds(upper_starts[b], upper_rows[b])] = pair(
+            jnp.concatenate(parts, axis=0)
+        ).astype(bf16)
     for b in range(depth):
         for mask in range(1 << b, 2 << b):
-            upper_copies.append(spread_upper(b, mask))
+            spread_upper(b, mask)
 
     gain = 3.0 / (length_scale * length_scale) * math.log2(math.e) ** 2
 
@@ -442,9 +424,6 @@
             + (1 - is_own - is_mate) * (2 * leaf_count + in_side)
         )
 
-    def kept(weights, flag):
-        return (weights.astype(f32) * flag.astype(f32)).astype(bf16)
-
     tiles = tests // TILE
 
     def near_block(slot, carry):
@@ -453,14 +432,12 @@
         value = (scaled + 1.0 / math.log(2.0)) * jnp.exp2(
             math.log2(variance * math.log(2.0)) - scaled
         )
-        blocks[slot] = value.astype(bf16)
+        rows = pl.ds(pl.multiple_of(slot * leaf_size, leaf_size), leaf_size)
+        blocks[rows] = value.astype(bf16)
         return carry
 
-    def add_block(slot):
-        total[...] = total[...] + nn(held[slot], blocks[slot])
-
     early = near * EARLY // 8
-    first = near * FIRST // 8
+    middle_slot = near * MIDDLE // 8
 
     mate_coords.wait()
     put_features(1, coord_window[0])
@@ -468,50 +445,51 @@
     put_features(2, coord_window[1])
     lax.fori_loop(0, early, near_block, 0)
 
-    for copy in copies:
-        copy.wait()
+    remote(received, received, round_send.at[0], round_recv.at[0], mate).wait()
     mines, others, mixed_far = [], [], []
+
+    def gathered(masks, k):
+        return unpair(
+            sum(received[unit_starts[mask] + k - (mask.bit_length() - 1)] for mask in masks)
+        )
+
     for k in range(depth):
         mine = flows[k]
         if k:
-            mine = mine + unpair(sum(received[mask, k].astype(f32) for mask in range(1, 1 << k)))
-        other = unpair(sum(received[mask, k].astype(f32) for mask in range(1 << k, 2 << k)))
+            mine = mine + gathered(range(1, 1 << k), k)
+        other = gathered(range(1 << k, 2 << k), k)
         mines.append(mine)
         others.append(other)
         mixed_far.append(triple(coupling[local + k], jnp.concatenate([mine, other], axis=0)))
 
     far_mix_high, far_mix_low = halves(jnp.concatenate(mixed_far, axis=0))
-    side_copies = []
     for leaf in range(leaf_count):
         upper_basis = bases[leaf][top:]
         state = solved[leaf] - tn(far_mix_high, upper_basis) - tn(far_mix_low, upper_basis)
-        pair_weights[leaf] = state.astype(bf16)
+        weight_window[leaf] = state.astype(bf16)
         copy = remote(
-            pair_weights.at[leaf],
-            side_weights.at[leaf],
-            side_send.at[leaf],
-            side_recv.at[leaf],
+            weight_window.at[leaf],
+            weight_window.at[2 * leaf_count + leaf],
+            side_send.at[0],
+            side_recv.at[0],
             side_safe,
         )
         pl.when(has_side)(copy.start)
-        side_copies.append(copy)
-    mate_weights = remote(
-        pair_weights.at[pl.ds(0, leaf_count)],
-        pair_weights.at[pl.ds(leaf_count, leaf_count)],
-        pair_send.at[0],
-        pair_recv.at[0],
-        mate,
-    )
+
+    def panel_of(index):
+        return weight_window.at[pl.ds(index * leaf_count, leaf_count)]
+
+    mate_weights = remote(panel_of(0), panel_of(1), pair_send.at[0], pair_recv.at[0], mate)
     mate_weights.start()
-
-    lax.fori_loop(early, first, near_block, 0)
-    for copy in upper_copies:
-        copy.wait()
+    side_weights = remote(panel_of(0), panel_of(2), side_send.at[0], side_recv.at[0], side_safe)
+
+    lax.fori_loop(early, middle_slot, near_block, 0)
+    remote(upper_received, upper_received, upper_send.at[0], upper_recv.at[0], mate).wait()
     far_rows = []
     for b in range(depth):
         flat = unpair(
             sum(
-                upper_received[pl.ds(upper_slots[b] + i * upper_rows[b], upper_rows[b])]
+                upper_received[pl.ds(upper_slots[b] + i * upper_rows[b], upper_rows[b])].astype(f32)
                 for i in range(1 << b)
             )
         )
@@ -523,52 +501,20 @@
     far_high, far_low = halves(jnp.concatenate(far_rows, axis=0))
     test_basis_copy.wait()
     test_basis = test_basis_ref[...].reshape(depth * rank, tests)
-    weigh = math.sqrt(near * leaf_size)
+    lax.fori_loop(middle_slot, near, near_block, 0)
+
+    mate_weights.wait()
+    pl.when(has_side)(side_weights.wait)
+    held = jnp.concatenate([weight_window[window_leaf(slot)] for slot in range(near)], axis=1)
     for tile in range(tiles):
         lanes = slice(tile * TILE, (tile + 1) * TILE)
-        total[:, lanes] = weigh * (
-            tn(far_high, test_basis[:, lanes]) + tn(far_low, test_basis[:, lanes])
-        )
-    mate_weights.wait()
-    for slot in range(near):
-        index = window_leaf(slot)
-        weights = pair_weights[jnp.minimum(index, 2 * leaf_count - 1)]
-        held[slot] = kept(weights, jnp.clip(2 * leaf_count - index, 0, 1))
-
-    added = 0
-    for slot in range(first, near):
-        upto = max(min(added + 2, slot), 0)
-        for done in range(added, upto):
-            add_block(done)
-        added = upto
-        near_block(slot, 0)
-    for slot in range(added, near):
-        add_block(slot)
-
-    places, arrived = [], []
-    for leaf in range(leaf_count):
-        pl.when(has_side)(side_copies[leaf].wait)
-    for leaf in range(leaf_count):
-        found, where = 0, 0
-        for slot in range(near):
-            away = window_leaf(slot) - 2 * leaf_count - leaf
-            match = jnp.clip(1 - away * away, 0, 1)
-            found = found + match
-            where = where + match * slot
-        arrived.append(kept(side_weights[leaf], jnp.clip(found, 0, 1)))
-        places.append(jnp.clip(where, 0, near - 1))
-    out_copies = []
-    for tile in range(tiles):
-        lanes = slice(tile * TILE, (tile + 1) * TILE)
-        value = total[:, lanes]
-        for weights, where in zip(arrived, places):
-            value = value + nn(weights, blocks[where, :, lanes])
-        out_ref[:, lanes] = (value * (1.0 / weigh)).astype(bf16)
-        copy = pltpu.make_async_copy(out_ref.at[:, lanes], out_hbm.at[:, lanes], out_sems.at[tile])
-        copy.start()
-        out_copies.append(copy)
-    for copy in out_copies:
-        copy.wait()
+        far_sum = tn(far_high, test_basis[:, lanes]) + tn(far_low, test_basis[:, lanes])
+        near_sum = nn(held, blocks[:, lanes])
+        out_ref[:, lanes] = (near_sum * (1.0 / math.sqrt(near * leaf_size)) + far_sum).astype(bf16)
+        pltpu.make_async_copy(
+            out_ref.at[:, lanes], out_hbm.at[:, lanes], out_sems.at[0]
+        ).start()
+    pltpu.make_async_copy(out_ref, out_hbm, out_sems.at[0]).wait()
 
 
 def shards(
@@ -592,6 +538,7 @@
     depth = levels - (leaf_count.bit_length() - 1)
     cross_starts, cross_slots = spans(depth, rank, "cross")[1:]
     upper_starts, upper_slots = spans(depth, rank, "upper")[1:]
+    units = sum((depth - b) << b for b in range(depth))
     anywhere = pl.BlockSpec(memory_space=pl.ANY)
     sems = pltpu.SemaphoreType.DMA
     operands = (
@@ -615,33 +562,29 @@
             pltpu.VMEM((columns, tests), bf16),
             pltpu.VMEM((cross_starts[-1], 4 * rank), f32),
             pltpu.VMEM((cross_slots[-1], 4 * rank), f32),
-            pltpu.VMEM((upper_starts[-1], 4 * rank), f32),
-            pltpu.VMEM((upper_slots[-1], 4 * rank), f32),
-            pltpu.VMEM((depth, rank // 2, 2 * columns), bf16),
-            pltpu.VMEM((panels, depth, rank // 2, 2 * columns), bf16),
+            pltpu.VMEM((upper_starts[-1], 4 * rank), bf16),
+            pltpu.VMEM((upper_slots[-1], 4 * rank), bf16),
+            pltpu.VMEM((depth, rank // 2, 2 * columns), f32),
+            pltpu.VMEM((units, rank // 2, 2 * columns), f32),
             pltpu.VMEM((2, 3, points), bf16),
             pltpu.VMEM((3 * leaf_count, FEATS, leaf_size), bf16),
             pltpu.VMEM((FEATS, tests), bf16),
-            pltpu.VMEM((near, leaf_size, tests), bf16),
-            pltpu.VMEM((2 * leaf_count, columns, leaf_size), bf16),
-            pltpu.VMEM((leaf_count, columns, leaf_size), bf16),
-            pltpu.VMEM((near, columns, leaf_size), bf16),
-            pltpu.VMEM((columns, tests), f32),
-            sems((8,)),
-            sems((leaf_count,)),
-            sems((tests // TILE,)),
-            sems((panels,)),
-            sems((panels,)),
-            sems((panels,)),
-            sems((panels,)),
-            sems((panels,)),
-            sems((panels,)),
+            pltpu.VMEM((near * leaf_size, tests), bf16),
+            pltpu.VMEM((3 * leaf_count, columns, leaf_size), bf16),
+            sems((9,)),
+            sems((1,)),
+            sems((1,)),
+            sems((1,)),
+            sems((1,)),
+            sems((1,)),
+            sems((1,)),
+            sems((1,)),
             sems((2,)),
             sems((2,)),
             sems((1,)),
             sems((1,)),
-            sems((leaf_count,)),
-            sems((leaf_count,)),
+            sems((1,)),
+            sems((1,)),
         ],
         compiler_params=pltpu.CompilerParams(
             collective_id=0, has_side_effects=True, vmem_limit_bytes=60 * 1024 * 1024

time: 28.7 us -> 26.8 us (0.934)
  Pallas kernels: 26.9 us -> 25 us
    pallas_call x1, Pallas kernels: 26.9 us -> 25 us  [shards(): pl.pallas_call(functools.partial(kernel, panels, sub_size), out_shape=jax...]
where the time goes in v3:
time: 26.8 us; the launch traced here: 26.7 us
  Pallas kernels  25 us (93%)
  local copies, waits for them, and re-layouts  1.67 us (6%)
    pallas_call x1, Pallas kernels, shards(): pl.pallas_call(functools.partial(kernel, panels, sub_size), out_shape=jax...  25 us
    unnamed x1, local copies, waits for them, and re-layouts  1.67 us

profile of v3, /device:TPU:0, one launch (start us, length us, event | category | flops | bytes accessed | tf_op | source)
XLA Modules:
  0.0 26.7 jit_solution(8494581941418209801)
XLA Ops:
  0.0 25.0 %shard_map.91 = bf16[64,2048]{1,0:T(8,128)(2,1)} custom-call(s32[1,2048]{1,0:T(1,128)} %order_hbm.1, bf16[64,2048]{1,0:T(8,128)(2,1)} %targets_hbm.1, bf16[4,512,512]{2,1,0:T(8,128)(2,1)} %inverse_hbm.1, bf16[6,32,2048]{2,1,0:T(8,128)(2,1)} %basis_hbm.1, f32[1,6,32,64]{3,2,1,0:T(8,128)} %coupling_hbm.1, bf16[3,2048]{1,0:T(4,128)(2,1)} %train_hbm.1, ...), custom_call_target="tpu_custom_call" | custom-call | tf_op jit(solution)/shard_map/pallas_call | solution.py:554
  25.0 1.7 %copy.11 = bf16[64,2048]{1,0:T(8,128)(2,1)} copy(bf16[64,2048]{1,0:T(8,128)(2,1)} %shard_map.91) | data formatting | bytes 524288

commit v4 on v3

--- a/solution.py
+++ b/solution.py
@@ -16,7 +16,7 @@
 TILE = 1024
 FEATS = 16
 EARLY = 4
-MIDDLE = 7
+MIDDLE = 6
 GUARD = 2.0**-12
 
 
@@ -121,6 +121,7 @@
     test_features,
     blocks,
     weight_window,
+    far_sum,
     load_sems,
     out_sems,
     cross_send,
@@ -335,6 +336,35 @@
         ]
     own = coefs[0]
 
+    gain = 3.0 / (length_scale * length_scale) * math.log2(math.e) ** 2
+
+    def norm(pos):
+        return gain * (pos[0:1] * pos[0:1] + pos[1:2] * pos[1:2] + pos[2:3] * pos[2:3])
+
+    def train_side(pos):
+        ones = jnp.ones((3, points), f32)
+        zero = jnp.zeros((1, points), f32)
+        parts = thirds(-2.0 * gain * pos) + thirds(norm(pos)) + [ones, zero + GUARD]
+        return jnp.concatenate(parts, axis=0).astype(bf16)
+
+    def put_features(panel, pos):
+        made = train_side(pos.astype(f32))
+        for leaf in range(leaf_count):
+            features[panel * leaf_count + leaf] = made[:, leaf * leaf_size : (leaf + 1) * leaf_size]
+
+    test_pos = test_ref[...].astype(f32)
+    ones = jnp.ones((3, tests), f32)
+    zero = jnp.zeros((1, tests), f32)
+    test_features[...] = jnp.concatenate(
+        [test_pos, test_pos, test_pos, ones] + thirds(norm(test_pos)) + [zero + 1.0], axis=0
+    ).astype(bf16)
+    put_features(0, train_ref[...])
+    for leaf in range(leaf_count):
+        mix_high, mix_low = halves(jnp.concatenate(mixes[leaf], axis=0))
+        solved[leaf] = (
+            solved[leaf] - tn(mix_high, bases[leaf][:top]) - tn(mix_low, bases[leaf][:top])
+        )
+
     remote(cross_received, cross_received, cross_send.at[0], cross_recv.at[0], mate).wait()
     summed = []
     for b in range(depth - 1):
@@ -357,7 +387,7 @@
             side_sum = first_half(crossing[j]) + sum(summed[b][j] for b in range(j + 1))
             rest = rest[rank:] - triple(side_sum, flows[j])
     for k in range(depth):
-        sent[k] = pair(flows[k])
+        sent[k] = pair(flows[k]).astype(bf16)
     unit_starts, units = [0], 0
     for mask in range(1, panels):
         unit_starts.append(units)
@@ -376,38 +406,6 @@
         upper_sent[pl.ds(upper_starts[b], upper_rows[b])] = pair(
             jnp.concatenate(parts, axis=0)
         ).astype(bf16)
-    for b in range(depth):
-        for mask in range(1 << b, 2 << b):
-            spread_upper(b, mask)
-
-    gain = 3.0 / (length_scale * length_scale) * math.log2(math.e) ** 2
-
-    def norm(pos):
-        return gain * (pos[0:1] * pos[0:1] + pos[1:2] * pos[1:2] + pos[2:3] * pos[2:3])
-
-    def train_side(pos):
-        ones = jnp.ones((3, points), f32)
-        zero = jnp.zeros((1, points), f32)
-        parts = thirds(-2.0 * gain * pos) + thirds(norm(pos)) + [ones, zero + GUARD]
-        return jnp.concatenate(parts, axis=0).astype(bf16)
-
-    def put_features(panel, pos):
-        made = train_side(pos.astype(f32))
-        for leaf in range(leaf_count):
-            features[panel * leaf_count + leaf] = made[:, leaf * leaf_size : (leaf + 1) * leaf_size]
-
-    test_pos = test_ref[...].astype(f32)
-    ones = jnp.ones((3, tests), f32)
-    zero = jnp.zeros((1, tests), f32)
-    test_features[...] = jnp.concatenate(
-        [test_pos, test_pos, test_pos, ones] + thirds(norm(test_pos)) + [zero + 1.0], axis=0
-    ).astype(bf16)
-    put_features(0, train_ref[...])
-    for leaf in range(leaf_count):
-        mix_high, mix_low = halves(jnp.concatenate(mixes[leaf], axis=0))
-        solved[leaf] = (
-            solved[leaf] - tn(mix_high, bases[leaf][:top]) - tn(mix_low, bases[leaf][:top])
-        )
 
     def within(place):
         return jnp.clip(place + 1, 0, 1) * jnp.clip(leaf_count - place, 0, 1)
@@ -443,14 +441,21 @@
     put_features(1, coord_window[0])
     pl.when(has_side)(side_coords.wait)
     put_features(2, coord_window[1])
-    lax.fori_loop(0, early, near_block, 0)
+    lax.fori_loop(0, early // 2, near_block, 0, unroll=2)
+    for b in range(depth):
+        for mask in range(1 << b, 2 << b):
+            spread_upper(b, mask)
+    lax.fori_loop(early // 2, early, near_block, 0, unroll=2)
 
     remote(received, received, round_send.at[0], round_recv.at[0], mate).wait()
     mines, others, mixed_far = [], [], []
 
     def gathered(masks, k):
         return unpair(
-            sum(received[unit_starts[mask] + k - (mask.bit_length() - 1)] for mask in masks)
+            sum(
+                received[unit_starts[mask] + k - (mask.bit_length() - 1)].astype(f32)
+                for mask in masks
+            )
         )
 
     for k in range(depth):
@@ -483,7 +488,7 @@
     mate_weights.start()
     side_weights = remote(panel_of(0), panel_of(2), side_send.at[0], side_recv.at[0], side_safe)
 
-    lax.fori_loop(early, middle_slot, near_block, 0)
+    lax.fori_loop(early, middle_slot, near_block, 0, unroll=2)
     remote(upper_received, upper_received, upper_send.at[0], upper_recv.at[0], mate).wait()
     far_rows = []
     for b in range(depth):
@@ -501,16 +506,18 @@
     far_high, far_low = halves(jnp.concatenate(far_rows, axis=0))
     test_basis_copy.wait()
     test_basis = test_basis_ref[...].reshape(depth * rank, tests)
-    lax.fori_loop(middle_slot, near, near_block, 0)
+    far_sum[...] = tn(far_high, test_basis) + tn(far_low, test_basis)
+    lax.fori_loop(middle_slot, near, near_block, 0, unroll=2)
 
     mate_weights.wait()
     pl.when(has_side)(side_weights.wait)
     held = jnp.concatenate([weight_window[window_leaf(slot)] for slot in range(near)], axis=1)
     for tile in range(tiles):
         lanes = slice(tile * TILE, (tile + 1) * TILE)
-        far_sum = tn(far_high, test_basis[:, lanes]) + tn(far_low, test_basis[:, lanes])
         near_sum = nn(held, blocks[:, lanes])
-        out_ref[:, lanes] = (near_sum * (1.0 / math.sqrt(near * leaf_size)) + far_sum).astype(bf16)
+        out_ref[:, lanes] = (
+            near_sum * (1.0 / math.sqrt(near * leaf_size)) + far_sum[:, lanes]
+        ).astype(bf16)
         pltpu.make_async_copy(
             out_ref.at[:, lanes], out_hbm.at[:, lanes], out_sems.at[0]
         ).start()
@@ -564,13 +571,14 @@
             pltpu.VMEM((cross_slots[-1], 4 * rank), f32),
             pltpu.VMEM((upper_starts[-1], 4 * rank), bf16),
             pltpu.VMEM((upper_slots[-1], 4 * rank), bf16),
-            pltpu.VMEM((depth, rank // 2, 2 * columns), f32),
-            pltpu.VMEM((units, rank // 2, 2 * columns), f32),
+            pltpu.VMEM((depth, rank // 2, 2 * columns), bf16),
+            pltpu.VMEM((units, rank // 2, 2 * columns), bf16),
             pltpu.VMEM((2, 3, points), bf16),
             pltpu.VMEM((3 * leaf_count, FEATS, leaf_size), bf16),
             pltpu.VMEM((FEATS, tests), bf16),
             pltpu.VMEM((near * leaf_size, tests), bf16),
             pltpu.VMEM((3 * leaf_count, columns, leaf_size), bf16),
+            pltpu.VMEM((columns, tests), f32),
             sems((9,)),
             sems((1,)),
             sems((1,)),

time: 26.8 us -> 26.3 us (0.981)
  Pallas kernels: 25 us -> 24.2 us
    pallas_call x1, Pallas kernels: 25 us -> 24.2 us  [shards(): pl.pallas_call(functools.partial(kernel, panels, sub_size), out_shape=jax...]
where the time goes in v4:
time: 26.3 us; the launch traced here: 25.9 us
  Pallas kernels  24.2 us (92%)
  local copies, waits for them, and re-layouts  1.67 us (6%)
    pallas_call x1, Pallas kernels, shards(): pl.pallas_call(functools.partial(kernel, panels, sub_size), out_shape=jax...  24.2 us
    unnamed x1, local copies, waits for them, and re-layouts  1.67 us

profile of v4, /device:TPU:0, one launch (start us, length us, event | category | flops | bytes accessed | tf_op | source)
XLA Modules:
  0.0 25.9 jit_solution(1913089042243083670)
XLA Ops:
  0.0 24.2 %shard_map.91 = bf16[64,2048]{1,0:T(8,128)(2,1)} custom-call(s32[1,2048]{1,0:T(1,128)} %order_hbm.1, bf16[64,2048]{1,0:T(8,128)(2,1)} %targets_hbm.1, bf16[4,512,512]{2,1,0:T(8,128)(2,1)} %inverse_hbm.1, bf16[6,32,2048]{2,1,0:T(8,128)(2,1)} %basis_hbm.1, f32[1,6,32,64]{3,2,1,0:T(8,128)} %coupling_hbm.1, bf16[3,2048]{1,0:T(4,128)(2,1)} %train_hbm.1, ...), custom_call_target="tpu_custom_call" | custom-call | tf_op jit(solution)/shard_map/pallas_call | solution.py:561
  24.2 1.7 %copy.11 = bf16[64,2048]{1,0:T(8,128)(2,1)} copy(bf16[64,2048]{1,0:T(8,128)(2,1)} %shard_map.91) | data formatting | bytes 524288

commit v5 on v4

--- a/solution.py
+++ b/solution.py
@@ -387,7 +387,7 @@
             side_sum = first_half(crossing[j]) + sum(summed[b][j] for b in range(j + 1))
             rest = rest[rank:] - triple(side_sum, flows[j])
     for k in range(depth):
-        sent[k] = pair(flows[k]).astype(bf16)
+        sent[k] = pair(flows[k])
     unit_starts, units = [0], 0
     for mask in range(1, panels):
         unit_starts.append(units)
@@ -453,7 +453,7 @@
     def gathered(masks, k):
         return unpair(
             sum(
-                received[unit_starts[mask] + k - (mask.bit_length() - 1)].astype(f32)
+                received[unit_starts[mask] + k - (mask.bit_length() - 1)]
                 for mask in masks
             )
         )
@@ -571,8 +571,8 @@
             pltpu.VMEM((cross_slots[-1], 4 * rank), f32),
             pltpu.VMEM((upper_starts[-1], 4 * rank), bf16),
             pltpu.VMEM((upper_slots[-1], 4 * rank), bf16),
-            pltpu.VMEM((depth, rank // 2, 2 * columns), bf16),
-            pltpu.VMEM((units, rank // 2, 2 * columns), bf16),
+            pltpu.VMEM((depth, rank // 2, 2 * columns), f32),
+            pltpu.VMEM((units, rank // 2, 2 * columns), f32),
             pltpu.VMEM((2, 3, points), bf16),
             pltpu.VMEM((3 * leaf_count, FEATS, leaf_size), bf16),
             pltpu.VMEM((FEATS, tests), bf16),

time: 26.3 us -> 26.7 us (1.015)
  Pallas kernels: 24.2 us -> 24.7 us
    pallas_call x1, Pallas kernels: 24.2 us -> 24.7 us  [shards(): pl.pallas_call(functools.partial(kernel, panels, sub_size), out_shape=jax...]
where the time goes in v5:
time: 26.7 us; the launch traced here: 26.4 us
  Pallas kernels  24.7 us (93%)
  local copies, waits for them, and re-layouts  1.67 us (6%)
    pallas_call x1, Pallas kernels, shards(): pl.pallas_call(functools.partial(kernel, panels, sub_size), out_shape=jax...  24.7 us
    unnamed x1, local copies, waits for them, and re-layouts  1.67 us

profile of v5, /device:TPU:0, one launch (start us, length us, event | category | flops | bytes accessed | tf_op | source)
XLA Modules:
  0.0 26.4 jit_solution(1493385010891817521)
XLA Ops:
  0.0 24.7 %shard_map.91 = bf16[64,2048]{1,0:T(8,128)(2,1)} custom-call(s32[1,2048]{1,0:T(1,128)} %order_hbm.1, bf16[64,2048]{1,0:T(8,128)(2,1)} %targets_hbm.1, bf16[4,512,512]{2,1,0:T(8,128)(2,1)} %inverse_hbm.1, bf16[6,32,2048]{2,1,0:T(8,128)(2,1)} %basis_hbm.1, f32[1,6,32,64]{3,2,1,0:T(8,128)} %coupling_hbm.1, bf16[3,2048]{1,0:T(4,128)(2,1)} %train_hbm.1, ...), custom_call_target="tpu_custom_call" | custom-call | tf_op jit(solution)/shard_map/pallas_call | solution.py:561
  24.7 1.7 %copy.11 = bf16[64,2048]{1,0:T(8,128)(2,1)} copy(bf16[64,2048]{1,0:T(8,128)(2,1)} %shard_map.91) | data formatting | bytes 524288
